TPU v7x, 32 devices: a whole 2x2x4 slice. The times are simulated.
32 devices in a mesh: cfg: 2 (over x), seq: 16 (over z, y, core).
Axes of the slice: x: 2, y: 2, z: 4, core: 2. Of those that a mesh axis runs over, the one named last changes fastest.
Arguments:
- hidden: bfloat16 [2, 2048, 1920], P('cfg', 'seq'), may hold values from -6 to 6
- modulation: float32 [6, 1920], replicated, may hold values from -3 to 3
- w_qkv: bfloat16 [3, 1920, 1024], replicated, may hold values from -0.125 to 0.125
- q_gain: float32 [64], replicated, may hold values from 1 to 13, as said below
- k_gain: float32 [64], replicated, may hold values from 1 to 13, as said below
- w_out: bfloat16 [1024, 1920], replicated, may hold values from -0.1875 to 0.1875
- text_count: int32 [2], P('cfg'), may hold values from 1 to 226
- block_order: int32 [16], P('seq'), may hold values from 0 to 15, each once
Outputs:
- guided: float32 [2048, 1920], P('seq', 'cfg')
Inputs may be any that keep to these rules, and one draw needn't show every extreme that they name: text_count[b] is how many of the 226 text positions of branch b (0 conditional, 1 unconditional) hold prompt tokens; keys at the other text positions are masked. Seq index j holds positions block_order[j] * 128 to block_order[j] * 128 + 127; every block appears once. `q_gain`: one gain for each of the 64 entries of a head, shared by all heads. `k_gain`: one gain for each of the 64 entries of a head, shared by all heads.
All inputs are finite; a program needn't handle non-finite values.
Results may differ from a plain program's by a relative error of at most 0.015.
The roundings to bfloat16 on the way count: a program that leaves them out, or rounds other values in their place, can miss the bound.
Values may be sent and summed in bfloat16 or wider, within the bound.
A program may use at most 256 MiB of HBM per device.

v0:
```python
import jax
import jax.numpy as jnp
from jax import lax
from jax.sharding import PartitionSpec as P

HEAD = 64
HEADS = 16
TXT = 226


GUIDANCE = 6.0
EPSILON = 1e-05
MASKED = -1000000000.0


def swapped(block, axis, apart):
    count = lax.axis_size(axis)
    route = []
    for low in range(count):
        high = low | 1 << apart
        if high != low and high < count:
            route += [(low, high), (high, low)]
    return lax.ppermute(block, axis, route)


def layer_normal(values_in):
    average = jnp.mean(values_in, axis=-1, keepdims=True)
    centred = values_in - average
    spread = jnp.mean(centred * centred, axis=-1, keepdims=True)
    return centred * lax.rsqrt(spread + EPSILON)


def modulated(states, is_text, modulation):
    normed = layer_normal(states.astype(jnp.float32))
    shift = jnp.where(is_text[:, None], modulation[3][None, :], modulation[0][None, :])
    scale = jnp.where(is_text[:, None], modulation[4][None, :], modulation[1][None, :])
    return (normed * (1.0 + scale) + shift).astype(jnp.bfloat16)


def head_normal(projected, gain):
    rows = projected.shape[0]
    heads_view = projected.reshape(rows, HEADS, HEAD)
    return (layer_normal(heads_view) * gain).reshape(rows, HEADS * HEAD).astype(jnp.bfloat16)


def projections(states, is_text, modulation, w_qkv, q_gain, k_gain):
    modded = modulated(states, is_text, modulation)
    query = head_normal(jnp.dot(modded, w_qkv[0], preferred_element_type=jnp.float32), q_gain)
    keys = head_normal(jnp.dot(modded, w_qkv[1], preferred_element_type=jnp.float32), k_gain)
    values = jnp.dot(modded, w_qkv[2], preferred_element_type=jnp.float32).astype(jnp.bfloat16)
    return (query, keys, values)


def fold_block(query_heads, carry, piece):
    highest, total, numer = carry
    keys_piece, values_piece, bias_piece = piece
    count = keys_piece.shape[0]
    key_heads = keys_piece.reshape(count, HEADS, HEAD)
    value_heads = values_piece.reshape(count, HEADS, HEAD)
    scores = jnp.einsum("qhd,khd->hqk", query_heads, key_heads, preferred_element_type=jnp.float32)
    scores = scores * HEAD ** (-0.5) + bias_piece.astype(jnp.float32)[None, None, :]
    new_high = jnp.maximum(highest, jnp.max(scores, axis=-1))
    expo = jnp.exp(scores - new_high[:, :, None])
    rescale = jnp.exp(highest - new_high)
    total = jnp.sum(expo, axis=-1)
    numer = numer * rescale.T[:, :, None] + jnp.einsum(
        "hqk,khd->qhd", expo.astype(jnp.bfloat16), value_heads, preferred_element_type=jnp.float32
    )
    return (new_high, total, numer)


def shards(hidden, modulation, w_qkv, q_gain, k_gain, w_out, text_count, block_order):
    states = hidden[0]
    tok_rows = states.shape[0]
    within = jnp.arange(tok_rows, dtype=jnp.int32)
    position = block_order[0] * tok_rows + within
    is_text = position < TXT
    keep = jnp.logical_or(position >= TXT, position < text_count[0])
    key_bias = jnp.where(keep, 0.0, MASKED).astype(jnp.bfloat16)
    query, keys, values = projections(states, is_text, modulation, w_qkv, q_gain, k_gain)
    query_heads = query.reshape(tok_rows, HEADS, HEAD)
    start_state = (
        jnp.full((HEADS, tok_rows), -1e30, jnp.float32),
        jnp.zeros((HEADS, tok_rows), jnp.float32),
        jnp.zeros((tok_rows, HEADS, HEAD), jnp.float32),
    )
    carry = fold_block(
        query_heads,
        start_state,
        (
            lax.all_gather(keys, "seq", axis=0, tiled=True),
            lax.all_gather(values, "seq", axis=0, tiled=True),
            lax.all_gather(key_bias, "seq", axis=0, tiled=True),
        ),
    )
    highest, total, numer = carry
    attended = (numer / total.T[:, :, None]).reshape(tok_rows, HEADS * HEAD).astype(jnp.bfloat16)
    gate = jnp.where(is_text[:, None], modulation[5][None, :], modulation[2][None, :])
    cfg_index = lax.axis_index("cfg")
    half_width = w_out.shape[1] // 2
    w_half = lax.dynamic_slice_in_dim(w_out, cfg_index * half_width, half_width, 1)
    gate_half = lax.dynamic_slice_in_dim(gate, cfg_index * half_width, half_width, 1)
    partner = swapped(attended, "cfg", 0)
    own_update = gate_half * jnp.dot(attended, w_half, preferred_element_type=jnp.float32)
    other_update = gate_half * jnp.dot(partner, w_half, preferred_element_type=jnp.float32)
    is_first = cfg_index == 0
    cond = jnp.where(is_first, own_update, other_update)
    uncond = jnp.where(is_first, other_update, own_update)
    return uncond + GUIDANCE * (cond - uncond)


def solution(mesh):
    in_specs = (P("cfg", "seq", None), P(), P(), P(), P(), P(), P("cfg"), P("seq"))
    out_specs = P("seq", "cfg")
    return jax.shard_map(shards, mesh=mesh, in_specs=in_specs, out_specs=out_specs, check_vma=False)
```

profile of v0, /device:TPU:0, one launch (start us, length us, event | category | flops | bytes accessed | tf_op | source)
XLA Modules:
  0.0 170.8 jit_solution(8093386982138254050)
XLA Ops:
  6.5 0.0 all-gather.4.cloned.1.call-start
  6.5 1.2 slice_reduce_fusion.5
  7.8 1.2 convert_reduce_fusion
  8.9 1.3 fusion.39
  10.9 5.6 %slice_bitcast_fusion.1 = (bf16[1024,1920]{0,1:T(8,128)(2,1)}, bf16[1024,1920]{0,1:T(8,128)(2,1)}) fusion(bf16[3,1920,1024]{2,1,0:T(8,128)(2,1)} %param.10), kind=kLoop, calls=%fused_computation.10 | loop fusion | bytes 15728640 | tf_op jit(solution)/shard_map/dot_general | solution.py:48
  16.6 0.0 copy-start.1
  16.6 6.3 %copy.16 = bf16[1024,1920]{1,0:T(8,128)(2,1)} copy(bf16[1024,1920]{0,1:T(8,128)(2,1)} %get-tuple-element.12) | data formatting | bytes 7864320 | tf_op jit(solution)/shard_map/dot_general | solution.py:49
  22.8 0.0 copy-done.1
  22.9 0.0 copy-start.3
  22.9 3.5 %fusion.60 = (f32[128,16]{0,1:T(8,128)S(1)}, f32[128,16,64]{0,2,1:T(8,128)S(1)}) fusion(bf16[16,64,1920]{2,1,0:T(8,128)(2,1)} %bitcast.65, f32[1920]{0:T(1024)S(1)} %get-tuple-element.9, f32[1920]{0:T(1024)S(1)} %get-tuple-element.10, f32[1920]{0:T(1024)S(1)} %get-tuple-element.6, f32[1920]{0:T(1024)S(1)} %get-tuple-element.7, ...), kind=kOutput, calls=%fused_computation.68 | convolution fusion | flops 505657344 | bytes 4988032 | tf_op jit(solution)/shard_map/dot_general | solution.py:49
  26.3 0.1 multiply_reduce_fusion
  26.4 0.0 copy-done.3
  26.4 0.8 multiply_convert_fusion
  27.3 0.0 all-gather.4.cloned.1.call-update
  27.3 0.0 all-gather.6.cloned.1.call-start
  27.3 3.7 %fusion.24 = bf16[128,1024]{1,0:T(8,128)(2,1)} fusion(bf16[3,1920,1024]{2,1,0:T(8,128)(2,1)} %param.10, bf16[1,128,1920]{2,1,0:T(8,128)(2,1)S(1)} %copy-done.1, f32[1920]{0:T(1024)S(1)} %get-tuple-element.9, f32[1920]{0:T(1024)S(1)} %get-tuple-element.10, f32[1920]{0:T(1024)S(1)} %get-tuple-element.6, f32[1920]{0:T(1024)S(1)} %get-tuple-element.7, ...), kind=kOutput, calls=%fused_computation.22 | convolution fusion | flops 505659392 | bytes 4717696 | tf_op jit(solution)/shard_map/dot_general | solution.py:50
  31.0 0.0 all-gather.6.cloned.1.call-update
  31.1 6.2 %copy.15 = bf16[1024,1920]{1,0:T(8,128)(2,1)} copy(bf16[1024,1920]{0,1:T(8,128)(2,1)} %get-tuple-element.11) | data formatting | bytes 7864320 | tf_op jit(solution)/shard_map/dot_general | solution.py:48
  38.0 23.4 %all-gather = bf16[16,1,128]{2,1,0:T(2,128)(2,1)S(1)} all-gather(bf16[1,1,128]{2,1,0:T(2,128)(2,1)S(1)} %fusion.52), channel_id=1, replica_groups=mesh['cfg'=2,'seq'=16] {'seq'}, dimensions={0}, use_global_device_ids=true | all-gather | bytes 4352 | tf_op jit(solution)/shard_map/all_gather | solution.py:93
  61.3 0.0 copy-start.2
  61.4 3.4 %fusion.61 = (f32[128,16]{0,1:T(8,128)S(1)}, f32[128,16,64]{0,2,1:T(8,128)S(1)}) fusion(bf16[16,64,1920]{2,1,0:T(8,128)(2,1)} %bitcast.64, f32[1920]{0:T(1024)S(1)} %get-tuple-element.9, f32[1920]{0:T(1024)S(1)} %get-tuple-element.10, f32[1920]{0:T(1024)S(1)} %get-tuple-element.6, f32[1920]{0:T(1024)S(1)} %get-tuple-element.7, ...), kind=kOutput, calls=%fused_computation.69 | convolution fusion | flops 505657344 | bytes 4988032 | tf_op jit(solution)/shard_map/dot_general | solution.py:48
  64.8 0.1 multiply_reduce_fusion.1
  64.9 17.7 %all-gather.4.cloned.1.call-done = bf16[2048,1024]{0,1:T(8,128)(2,1)} async-done(((bf16[128,1024]{0,1:T(8,128)(2,1)}), bf16[2048,1024]{0,1:T(8,128)(2,1)}) %all-gather.4.cloned.1.call-update) | async-done | bytes 4194320 | tf_op jit(solution)/shard_map/all_gather | solution.py:91
  82.6 0.0 copy-done.2
  82.6 4.5 %fusion = (f32[16,128]{1,0:T(8,128)S(1)}, f32[16,128,2048]{2,1,0:T(8,128)S(1)}) fusion(f32[2048]{0:T(1024)S(1)} %bitcast.69, bf16[2048,16,64]{0,2,1:T(8,128)(2,1)} %bitcast.62, f32[128,16,64]{0,2,1:T(8,128)S(1)} %get-tuple-element.18, f32[64]{0:T(128)S(1)} %copy-done.2, f32[128,16]{0,1:T(8,128)S(1)} %add_rsqrt_fusion.1, ...), kind=kOutput, calls=%fused_computation.2 | convolution fusion | flops 549976064 | bytes 21528832 | tf_op jit(solution)/shard_map/qhd,khd->hqk/dot_general | solution.py:60
  87.2 0.0 copy-start
  87.2 5.8 %copy-done = f32[16,128,2048]{2,1,0:T(8,128)} copy-done((f32[16,128,2048]{2,1,0:T(8,128)}, f32[16,128,2048]{2,1,0:T(8,128)S(1)}, u32[]{:S(2)}) %copy-start) | copy-done | bytes 16777240
  93.0 3.8 %fusion.1 = f32[16,128]{1,0:T(8,128)S(1)} fusion(f32[16,128,2048]{2,1,0:T(8,128)S(1)} %get-tuple-element.20, f32[16,128]{1,0:T(8,128)S(1)} %get-tuple-element.14, f32[2048]{0:T(1024)S(1)} %bitcast.70), kind=kLoop, calls=%fused_computation.3 | loop fusion | flops 16775168 | bytes 16801792 | tf_op jit(solution)/shard_map/reduce_sum | solution.py:65
  96.8 36.6 %all-gather.6.cloned.1.call-done = bf16[2048,1024]{1,0:T(8,128)(2,1)} async-done(((bf16[128,1024]{1,0:T(8,128)(2,1)}), bf16[2048,1024]{1,0:T(8,128)(2,1)}) %all-gather.6.cloned.1.call-update) | async-done | bytes 4194320 | tf_op jit(solution)/shard_map/all_gather | solution.py:92
  133.4 6.5 %copy.17 = bf16[2048,1024]{0,1:T(8,128)(2,1)} copy(bf16[2048,1024]{1,0:T(8,128)(2,1)} %all-gather.6.cloned.1.call-done) | data formatting | bytes 8388608 | tf_op jit(solution)/shard_map/all_gather | solution.py:92
  139.9 11.1 %fusion.30 = bf16[128,16,64]{0,2,1:T(8,128)(2,1)S(1)} fusion(bf16[2048,16,64]{0,2,1:T(8,128)(2,1)} %bitcast.63, f32[16,128,2048]{2,1,0:T(8,128)} %copy-done, f32[16,128]{1,0:T(8,128)S(1)} %get-tuple-element.14, f32[2048]{0:T(1024)S(1)} %bitcast.71, f32[128,16]{0,1:T(8,128)S(1)} %bitcast.72, f32[128,16]{0,1:T(8,128)S(1)} %get-tuple-element.13), kind=kOutput, calls=%fused_computation.24 | convolution fusion | flops 554041344 | bytes 21266432 | tf_op jit(solution)/shard_map/hqk,khd->qhd/dot_general | solution.py:66
  151.0 1.5 collective-permute-start
  152.5 0.1 dynamic-slice
  152.6 0.1 dynamic-slice.1
  152.7 3.7 %fusion.18 = f32[128,960]{0,1:T(8,128)S(1)} fusion(bf16[128,1024]{0,1:T(8,128)(2,1)S(1)} %bitcast.68, bf16[1024,1920]{1,0:T(8,128)(2,1)} %param.13, s32[]{:T(128)S(6)} %select_n.50, f32[960]{0:T(1024)S(1)} %dynamic-slice.1, f32[960]{0:T(1024)S(1)} %dynamic-slice, pred[128]{0:T(512)(128)(4,1)S(1)} %fusion.53), kind=kOutput, calls=%fused_computation.20 | convolution fusion | flops 251904000 | bytes 2858628 | tf_op jit(solution)/shard_map/dot_general | solution.py:104
  156.4 3.2 %collective-permute-done = bf16[128,1024]{0,1:T(8,128)(2,1)S(1)} collective-permute-done((bf16[128,1024]{0,1:T(8,128)(2,1)S(1)}, bf16[128,1024]{0,1:T(8,128)(2,1)S(1)}, u32[]{:S(2)}, u32[]{:S(2)}) %collective-permute-start) | collective-permute-done | bytes 262176 | tf_op jit(solution)/shard_map/ppermute | solution.py:23
  159.5 4.5 %multiply_add_fusion.1 = f32[128,960]{0,1:T(8,128)} fusion(f32[128,960]{0,1:T(8,128)S(1)} %fusion.18, bf16[128,1024]{0,1:T(8,128)(2,1)S(1)} %collective-permute-done, bf16[1024,1920]{1,0:T(8,128)(2,1)} %param.13, s32[]{:T(128)S(6)} %select_n.50, f32[960]{0:T(1024)S(1)} %dynamic-slice.1, f32[960]{0:T(1024)S(1)} %dynamic-slice, ...), kind=kOutput, calls=%fused_computation.41 | convolution fusion | flops 252518400 | bytes 3350149 | tf_op jit(solution)/shard_map/dot_general | solution.py:105
  (10 shorter events, 0.1 us)
Async XLA Ops:
  6.5 76.1 %all-gather.4.cloned.1.call-start = ((), (), s32[]{:S(2)}) async-start(), calls=%async_computation | async-start | bytes 4456448 | tf_op jit(solution)/shard_map/all_gather | solution.py:91
  16.6 6.3 %copy-start.1 = (bf16[1,128,1920]{2,1,0:T(8,128)(2,1)S(1)}, bf16[1,128,1920]{2,1,0:T(8,128)(2,1)}, u32[]{:S(2)}) copy-start(bf16[1,128,1920]{2,1,0:T(8,128)(2,1)} %param.8) | copy-start | bytes 1474564
  22.9 3.6 %copy-start.3 = (f32[64]{0:T(128)S(1)}, f32[64]{0:T(128)}, u32[]{:S(2)}) copy-start(f32[64]{0:T(128)} %param.12) | copy-start | bytes 772
  27.3 106.1 %all-gather.6.cloned.1.call-start = ((), (), s32[]{:S(2)}) async-start(), calls=%async_computation.1 | async-start | bytes 4456448 | tf_op jit(solution)/shard_map/all_gather | solution.py:92
  61.3 21.3 %copy-start.2 = (f32[64]{0:T(128)S(1)}, f32[64]{0:T(128)}, u32[]{:S(2)}) copy-start(f32[64]{0:T(128)} %param.11) | copy-start | bytes 772
  87.2 5.8 %copy-start = (f32[16,128,2048]{2,1,0:T(8,128)}, f32[16,128,2048]{2,1,0:T(8,128)S(1)}, u32[]{:S(2)}) copy-start(f32[16,128,2048]{2,1,0:T(8,128)S(1)} %get-tuple-element.20) | copy-start | bytes 50331652
  151.0 8.5 %collective-permute-start = (bf16[128,1024]{0,1:T(8,128)(2,1)S(1)}, bf16[128,1024]{0,1:T(8,128)(2,1)S(1)}, u32[]{:S(2)}, u32[]{:S(2)}) collective-permute-start(bf16[128,1024]{0,1:T(8,128)(2,1)S(1)} %bitcast.67), channel_id=1, source_target_pairs={{0,16},{16,0},{1,17},{17,1},{2,18},{18,2},{3,19},{19,3},{4,20},{20... | collective-permute-start | bytes 786440 | tf_op jit(solution)/shard_map/ppermute | solution.py:23
Sparse Core Ops, SparseCore 0:
  27.4 55.1 all-gather.3
  84.8 48.5 all-gather.5
where the time goes:
time: 172 us; the launch traced here: 171 us
  waiting for transfers between devices  57.5 us (33%)
  matrix products  34.4 us (20%)
  local copies, waits for them, and re-layouts  31.8 us (18%)
  blocking collectives  23.4 us (14%)
  between operations  14.8 us (9%)
  other arithmetic  7.31 us (4%)
    all_gather x1, waiting for transfers between devices, shards(): lax.all_gather(values, 'seq', axis=0, tiled=True)  36.6 us
    all_gather x1, blocking collectives, shards(): lax.all_gather(key_bias, 'seq', axis=0, tiled=True)  23.4 us
    all_gather x1, waiting for transfers between devices, shards(): lax.all_gather(keys, 'seq', axis=0, tiled=True)  17.7 us
    dot_general x2, local copies, waits for them, and re-layouts, projections(): jnp.dot(modded, w_qkv[0], preferred_element_type=jnp.float32)  11.9 us
    dot_general x1, matrix products, fold_block(): jnp.einsum('hqk,khd->qhd', expo.astype(jnp.bfloat16), value_heads, prefer...  11.1 us
    all_gather x1, local copies, waits for them, and re-layouts, shards(): lax.all_gather(values, 'seq', axis=0, tiled=True)  6.51 us
    dot_general x1, local copies, waits for them, and re-layouts, projections(): jnp.dot(modded, w_qkv[1], preferred_element_type=jnp.float32)  6.29 us
    unnamed x8, local copies, waits for them, and re-layouts  5.81 us
  transfers between devices with their start and end apart: 3, of which 3 were waited for; matrix products, arithmetic and copies ran while one was open for 15% of the time, Pallas kernels for 0%

commit v1 on v0

--- a/solution.py
+++ b/solution.py
@@ -1,6 +1,10 @@
+import functools
+
 import jax
 import jax.numpy as jnp
 from jax import lax
+from jax.experimental import pallas as pl
+from jax.experimental.pallas import tpu as pltpu
 from jax.sharding import PartitionSpec as P
 
 HEAD = 64
@@ -109,7 +113,286 @@
     return uncond + GUIDANCE * (cond - uncond)
 
 
+LANES = 128
+GROUPS = 4
+MESH = pl.DeviceIdType.MESH
+
+
+def flip(bit, other):
+    return lax.rem(bit + other, 2)
+
+
+def pair_normal(x, low):
+    def halves(y):
+        first = jnp.sum(jnp.where(low, y, 0.0), axis=-1, keepdims=True)
+        second = jnp.sum(jnp.where(low, 0.0, y), axis=-1, keepdims=True)
+        return jnp.where(low, first, second) * (1.0 / HEAD)
+
+    centred = x - halves(x)
+    return centred * lax.rsqrt(halves(centred * centred) + EPSILON)
+
+
+def turned(x):
+    return pltpu.roll(x, HEAD, 1)
+
+
+def fused(n, count_ref, block_ref, hidden_ref, mod_ref, w_ref, qg_ref, kg_ref, wo_ref, out_ref,
+          w_buf, wo_buf, modded, kv_out, kv_in, q_out, q_in, bias_out, bias_in, bias_row,
+          att_out, att_in, att_far, stacked,
+          w_sem, wo_sem, kv_s, kv_r, q_s, q_r, b_s, b_r, a_s, a_r, f_s, f_r):
+    me = lax.axis_index("seq")
+    cfg = lax.axis_index("cfg")
+    rows, width = hidden_ref.shape
+    half_rows = rows // 2
+    half = width // 2
+    wide = wo_buf.shape[1]
+    cols = w_buf.shape[3]
+    heads_here = cols // HEAD
+    plane = lax.div(me, GROUPS)
+    plane_high, plane_low = lax.div(plane, 2), lax.rem(plane, 2)
+
+    def group(i):
+        high = 1 - lax.div(i, 2)
+        lowbit = flip(lax.div(i, 2), lax.rem(i, 2))
+        return 2 * flip(plane_high, high) + flip(plane_low, lowbit)
+
+    def weight(kind, i):
+        start = pl.multiple_of(group(i) * cols, cols)
+        return pltpu.make_async_copy(
+            w_ref.at[kind, :, pl.ds(start, cols)], w_buf.at[kind, i], w_sem.at[kind, i])
+
+    column = pl.multiple_of(cfg * (width - wide), LANES)
+    out_weight = pltpu.make_async_copy(wo_ref.at[:, pl.ds(column, wide)], wo_buf, wo_sem)
+
+    barrier = pltpu.get_barrier_semaphore()
+    for j in range(1, n):
+        pl.semaphore_signal(barrier, inc=1, device_id={"seq": lax.rem(me + j, n)}, device_id_type=MESH)
+    pl.semaphore_signal(barrier, inc=1, device_id={"cfg": 1 - cfg}, device_id_type=MESH)
+    for i in range(GROUPS):
+        weight(1, i).start()
+        weight(2, i).start()
+    for i in range(GROUPS):
+        weight(0, i).start()
+    out_weight.start()
+
+    def send(src, dst, to, s_sem, r_sem):
+        @pl.when(to != me)
+        def _():
+            pltpu.make_async_remote_copy(
+                src_ref=src.at[to], dst_ref=dst.at[me], send_sem=s_sem.at[to], recv_sem=r_sem.at[me],
+                device_id={"seq": to}, device_id_type=MESH).start()
+
+        @pl.when(to == me)
+        def _():
+            pltpu.make_async_copy(src.at[to], dst.at[me], r_sem.at[me]).start()
+
+    def arrived(dst, source, r_sem):
+        pltpu.make_async_copy(dst.at[source], dst.at[source], r_sem.at[source]).wait()
+
+    def sent(src, to, s_sem):
+        @pl.when(to != me)
+        def _():
+            pltpu.make_async_copy(src.at[to], src.at[to], s_sem.at[to]).wait()
+
+    block = block_ref[0]
+    count = count_ref[0]
+    across = block * rows + lax.broadcasted_iota(jnp.int32, (1, rows), 1)
+    keep = jnp.logical_or(across >= TXT, across < count)
+    bias_out[0:n] = jnp.broadcast_to(jnp.where(keep, 0.0, MASKED)[None], (n, 1, rows)).astype(jnp.bfloat16).astype(jnp.float32)
+
+    mod = mod_ref[...]
+    down = block * rows + lax.broadcasted_iota(jnp.int32, (rows, 1), 0)
+    is_text = down < TXT
+    normed = layer_normal(hidden_ref[...].astype(jnp.float32))
+    shift = jnp.where(is_text, mod[3:4, :], mod[0:1, :])
+    scale = jnp.where(is_text, mod[4:5, :], mod[1:2, :])
+    modded[...] = (normed * (1.0 + scale) + shift).astype(jnp.bfloat16)
+
+    low = lax.broadcasted_iota(jnp.int32, (1, LANES), 1) < HEAD
+    pl.semaphore_wait(barrier, n)
+
+    def send_bias(j, carry):
+        send(bias_out, bias_in, j, b_s, b_r)
+        return carry
+
+    lax.fori_loop(0, n, send_bias, 0)
+
+    k_gain = kg_ref[...]
+    q_gain = qg_ref[...] * HEAD ** (-0.5)
+
+    def project_kv(i, carry):
+        weight(1, i).wait()
+        weight(2, i).wait()
+        first = group(i) * heads_here
+        x = modded[...]
+        k_all = jnp.dot(x, w_buf[1, i], preferred_element_type=jnp.float32)
+        v_all = jnp.dot(x, w_buf[2, i], preferred_element_type=jnp.float32)
+        for p in range(heads_here // 2):
+            k = pair_normal(k_all[:, p * LANES:(p + 1) * LANES], low) * k_gain
+            v = v_all[:, p * LANES:(p + 1) * LANES]
+            kv_out[first + 2 * p] = jnp.where(low, k, turned(v)).astype(jnp.bfloat16)
+            kv_out[first + 2 * p + 1] = jnp.where(low, turned(k), v).astype(jnp.bfloat16)
+        for h in range(heads_here):
+            send(kv_out, kv_in, first + h, kv_s, kv_r)
+        return carry
+
+    lax.fori_loop(0, GROUPS, project_kv, 0)
+
+    def project_q(i, carry):
+        weight(0, i).wait()
+        first = group(i) * heads_here
+        q_all = jnp.dot(modded[...], w_buf[0, i], preferred_element_type=jnp.float32)
+        for p in range(heads_here // 2):
+            q = pair_normal(q_all[:, p * LANES:(p + 1) * LANES], low) * q_gain
+            top, bottom = q[:half_rows], q[half_rows:]
+            q_out[first + 2 * p] = jnp.where(low, top, turned(bottom)).astype(jnp.bfloat16)
+            q_out[first + 2 * p + 1] = jnp.where(low, turned(top), bottom).astype(jnp.bfloat16)
+        for h in range(heads_here):
+            send(q_out, q_in, first + h, q_s, q_r)
+        return carry
+
+    lax.fori_loop(0, GROUPS, project_q, 0)
+
+    for j in range(n):
+        arrived(bias_in, j, b_r)
+    for j in range(n):
+        bias_row[:, j * rows:(j + 1) * rows] = jnp.broadcast_to(bias_in[j], (8, rows))
+
+    def wait_kv(j, carry):
+        arrived(kv_in, j, kv_r)
+        return carry
+
+    lax.fori_loop(0, n, wait_kv, 0)
+
+    chip = lax.div(me, 2)
+
+    def pair_of(k):
+        c0, c1, c2 = lax.rem(chip, 2), lax.rem(lax.div(chip, 2), 2), lax.div(chip, 4)
+        k0, k1, k2 = lax.rem(k, 2), lax.rem(lax.div(k, 2), 2), lax.div(k, 4)
+        return 4 * flip(c2, k2) + 2 * flip(c1, k1) + flip(c0, k0)
+
+    def forward(k):
+        for i in range(2):
+            h = 2 * pair_of(k) + i
+            arrived(att_in, h, a_r)
+            pltpu.make_async_remote_copy(
+                src_ref=att_in.at[h], dst_ref=att_far.at[h], send_sem=f_s.at[h], recv_sem=f_r.at[h],
+                device_id={"cfg": 1 - cfg}, device_id_type=MESH).start()
+
+    def attend(k, carry):
+        base = 2 * pair_of(k)
+        parts = []
+        for i in range(2):
+            arrived(q_in, base + i, q_r)
+            folded = q_in[base + i].astype(jnp.float32)
+            parts += [jnp.where(low, folded, 0.0), jnp.where(low, turned(folded), 0.0)]
+        query = jnp.concatenate(parts, axis=0).astype(jnp.bfloat16)
+        keys = kv_in[...].reshape(n * rows, LANES)
+        scores = lax.dot_general(query, keys, (((1,), (1,)), ((), ())), preferred_element_type=jnp.float32)
+        scores = scores + bias_row[0:1, :]
+        expo = jnp.exp(scores - jnp.max(scores, axis=-1, keepdims=True))
+        total = jnp.sum(expo, axis=-1, keepdims=True)
+        numer = jnp.dot(expo.astype(jnp.bfloat16), keys, preferred_element_type=jnp.float32)
+        result = numer / total
+        for i in range(2):
+            top = result[i * rows:i * rows + half_rows]
+            bottom = result[i * rows + half_rows:(i + 1) * rows]
+            att_out[base + i] = jnp.where(low, turned(top), bottom).astype(jnp.bfloat16)
+            send(att_out, att_in, base + i, a_s, a_r)
+
+        @pl.when(k >= 2)
+        def _():
+            forward(k - 2)
+
+        return carry
+
+    steps = n // 2
+    lax.fori_loop(0, steps, attend, 0)
+    forward(steps - 2)
+    forward(steps - 1)
+    out_weight.wait()
+
+    def assemble(source, at):
+        for p in range(n // 2):
+            a = source[2 * p].astype(jnp.float32)
+            b = source[2 * p + 1].astype(jnp.float32)
+            span = slice(p * LANES, (p + 1) * LANES)
+            stacked[at:at + half_rows, span] = jnp.where(low, a, turned(b)).astype(jnp.bfloat16)
+            stacked[at + half_rows:at + rows, span] = jnp.where(low, turned(a), b).astype(jnp.bfloat16)
+
+    assemble(att_in, 0)
+    for h in range(n):
+        arrived(att_far, h, f_r)
+    assemble(att_far, rows)
+    both = jnp.dot(stacked[...], wo_buf[...], preferred_element_type=jnp.float32)
+    is_first = cfg == 0
+    gate_text = jnp.where(is_first, mod[5:6, :wide], mod[5:6, width - wide:])
+    gate_video = jnp.where(is_first, mod[2:3, :wide], mod[2:3, width - wide:])
+    gate = jnp.where(is_text, gate_text, gate_video)
+    own, other = gate * both[:rows], gate * both[rows:]
+    cond = jnp.where(is_first, own, other)
+    uncond = jnp.where(is_first, other, own)
+    guided = uncond + GUIDANCE * (cond - uncond)
+    excess = wide - half
+    guided = jnp.where(is_first, guided, pltpu.roll(guided, half, 1)) if excess else guided
+    out_ref[...] = guided[:, :half]
+
+    def finish(j, carry):
+        sent(bias_out, j, b_s)
+        sent(kv_out, j, kv_s)
+        sent(q_out, j, q_s)
+        sent(att_out, j, a_s)
+        pltpu.make_async_copy(att_in.at[j], att_in.at[j], f_s.at[j]).wait()
+        return carry
+
+    lax.fori_loop(0, n, finish, 0)
+
+
+def whole_kernel(hidden, modulation, w_qkv, q_gain, k_gain, w_out, text_count, block_order):
+    n = lax.axis_size("seq")
+    states = hidden[0]
+    rows, width = states.shape
+    features = w_out.shape[0]
+    cols = features // GROUPS
+    half = width // 2
+    wide = -(-half // LANES) * LANES
+    bf, f32 = jnp.bfloat16, jnp.float32
+    vmem = pl.BlockSpec(memory_space=pltpu.VMEM)
+    smem = pl.BlockSpec(memory_space=pltpu.SMEM)
+    hbm = pl.BlockSpec(memory_space=pl.ANY)
+    dma = pltpu.SemaphoreType.DMA
+    double = lambda gain: jnp.concatenate([gain, gain])[None, :]
+    return pl.pallas_call(
+        functools.partial(fused, n),
+        out_shape=jax.ShapeDtypeStruct((rows, half), f32),
+        in_specs=[smem, smem, vmem, vmem, hbm, vmem, vmem, hbm],
+        out_specs=vmem,
+        scratch_shapes=[
+            pltpu.VMEM((3, GROUPS, width, cols), bf),
+            pltpu.VMEM((features, wide), bf),
+            pltpu.VMEM((rows, width), bf),
+            pltpu.VMEM((n, rows, LANES), bf),
+            pltpu.VMEM((n, rows, LANES), bf),
+            pltpu.VMEM((n, rows // 2, LANES), bf),
+            pltpu.VMEM((n, rows // 2, LANES), bf),
+            pltpu.VMEM((n + 8, 1, rows), f32),
+            pltpu.VMEM((n + 8, 1, rows), f32),
+            pltpu.VMEM((8, n * rows), f32),
+            pltpu.VMEM((n, rows // 2, LANES), bf),
+            pltpu.VMEM((n, rows // 2, LANES), bf),
+            pltpu.VMEM((n, rows // 2, LANES), bf),
+            pltpu.VMEM((2 * rows, features), bf),
+            dma((3, GROUPS)),
+            dma,
+        ] + [dma((n,))] * 10,
+        compiler_params=pltpu.CompilerParams(
+            collective_id=0, has_side_effects=True, vmem_limit_bytes=60 * 1024 * 1024),
+    )(text_count, block_order, states, modulation, w_qkv, double(q_gain), double(k_gain), w_out)
+
+
 def solution(mesh):
     in_specs = (P("cfg", "seq", None), P(), P(), P(), P(), P(), P("cfg"), P("seq"))
     out_specs = P("seq", "cfg")
-    return jax.shard_map(shards, mesh=mesh, in_specs=in_specs, out_specs=out_specs, check_vma=False)
+    one_head_each = mesh.shape["seq"] == HEADS and mesh.shape["cfg"] == 2
+    body = whole_kernel if one_head_each else shards
+    return jax.shard_map(body, mesh=mesh, in_specs=in_specs, out_specs=out_specs, check_vma=False)

time: 172 us -> 50.2 us (0.29)
  waiting for transfers between devices: 57.5 us -> 0 us
  Pallas kernels: 0 us -> 45.3 us
  matrix products: 34.4 us -> 0 us
  local copies, waits for them, and re-layouts: 31.8 us -> 2.02 us
  blocking collectives: 23.4 us -> 0 us
  between operations: 14.8 us -> 1.31 us
  other arithmetic: 7.31 us -> 1.32 us
    all_gather x2 -> x0, waiting for transfers between devices: 54.3 us -> none  [the longest x1 36.6 us: shards(): lax.all_gather(values, 'seq', axis=0, tiled=True)]
    pallas_call x0 -> x1, Pallas kernels: none -> 45.3 us  [whole_kernel(): pl.pallas_call(functools.partial(fused, n), out_shape=jax.ShapeDtypeStruc...]
    dot_general x7 -> x0, matrix products: 34.4 us -> none  [the longest x1 11.1 us: fold_block(): jnp.einsum('hqk,khd->qhd', expo.astype(jnp.bfloat16), value_heads, prefer...]
    all_gather x1 -> x0, blocking collectives: 23.4 us -> none  [shards(): lax.all_gather(key_bias, 'seq', axis=0, tiled=True)]
    dot_general x3 -> x0, local copies, waits for them, and re-layouts: 18.1 us -> none  [the longest x2 11.9 us: projections(): jnp.dot(modded, w_qkv[0], preferred_element_type=jnp.float32)]
    all_gather x1 -> x0, local copies, waits for them, and re-layouts: 6.51 us -> none  [shards(): lax.all_gather(values, 'seq', axis=0, tiled=True)]
    reduce_sum x5 -> x0, other arithmetic: 6.41 us -> none  [the longest x1 3.78 us: fold_block(): total = jnp.sum(expo, axis=-1)]
    unnamed x8 -> x0, local copies, waits for them, and re-layouts: 5.81 us -> none
  transfers between devices with their start and end apart: 3 -> 0, of which waited for: 3 -> 0; matrix products, arithmetic and copies ran while one was open for 15% -> 0% of each run, Pallas kernels for 0% -> 0%
where the time goes in v1:
time: 50.2 us; the launch traced here: 50 us
  Pallas kernels  45.3 us (90%)
  local copies, waits for them, and re-layouts  2.02 us (4%)
  other arithmetic  1.32 us (3%)
  between operations  1.31 us (3%)
    pallas_call x1, Pallas kernels, whole_kernel(): pl.pallas_call(functools.partial(fused, n), out_shape=jax.ShapeDtypeStruc...  45.3 us
    pallas_call x1, local copies, waits for them, and re-layouts, whole_kernel(): pl.pallas_call(functools.partial(fused, n), out_shape=jax.ShapeDtypeStruc...  2.02 us
    broadcast_in_dim x1, other arithmetic, whole_kernel(): double = lambda gain: jnp.concatenate([gain, gain])[None, :]  1.32 us

profile of v1, /device:TPU:0, one launch (start us, length us, event | category | flops | bytes accessed | tf_op | source)
XLA Modules:
  0.0 50.0 jit_solution(15077264683599628902)
XLA Ops:
  1.3 1.3 %maximum_bitcast_fusion = (f32[1,128]{1,0:T(1,128)}, f32[1,128]{1,0:T(1,128)}) fusion(f32[64]{0:T(128)} %param.11, f32[64]{0:T(128)} %param.12), kind=kLoop, calls=%fused_computation | loop fusion | flops 256 | bytes 1536 | tf_op jit(solution)/shard_map/broadcast_in_dim | solution.py:364
  2.6 45.3 %shard_map.82 = f32[128,960]{1,0:T(8,128)} custom-call(s32[1]{0:T(128)S(6)} %copy.10.count_ref, s32[1]{0:T(128)S(6)} %copy.11.block_ref, bf16[128,1920]{1,0:T(8,128)(2,1)} %bitcast.5, f32[6,1920]{1,0:T(8,128)} %mod_ref.1, bf16[3,1920,1024]{2,1,0:T(8,128)(2,1)} %w_ref.1, f32[1,128]{1,0:T(1,128)} %get-tuple-element.5.qg_ref, ...), custom_call_target="tpu_custom_call" | custom-call | tf_op jit(solution)/shard_map/pallas_call | solution.py:365
  47.9 2.0 %copy.9 = f32[128,960]{0,1:T(8,128)} copy(f32[128,960]{1,0:T(8,128)} %shard_map.82) | data formatting | bytes 983040 | tf_op jit(solution)/shard_map/pallas_call | solution.py:365

commit v2 on v1

--- a/solution.py
+++ b/solution.py
@@ -266,7 +266,8 @@
 
     chip = lax.div(me, 2)
 
-    def pair_of(k):
+    def pair_of(step):
+        k = n // 2 - 1 - step
         c0, c1, c2 = lax.rem(chip, 2), lax.rem(lax.div(chip, 2), 2), lax.div(chip, 4)
         k0, k1, k2 = lax.rem(k, 2), lax.rem(lax.div(k, 2), 2), lax.div(k, 4)
         return 4 * flip(c2, k2) + 2 * flip(c1, k1) + flip(c0, k0)
@@ -286,14 +287,26 @@
             arrived(q_in, base + i, q_r)
             folded = q_in[base + i].astype(jnp.float32)
             parts += [jnp.where(low, folded, 0.0), jnp.where(low, turned(folded), 0.0)]
-        query = jnp.concatenate(parts, axis=0).astype(jnp.bfloat16)
         keys = kv_in[...].reshape(n * rows, LANES)
-        scores = lax.dot_general(query, keys, (((1,), (1,)), ((), ())), preferred_element_type=jnp.float32)
-        scores = scores + bias_row[0:1, :]
-        expo = jnp.exp(scores - jnp.max(scores, axis=-1, keepdims=True))
-        total = jnp.sum(expo, axis=-1, keepdims=True)
-        numer = jnp.dot(expo.astype(jnp.bfloat16), keys, preferred_element_type=jnp.float32)
-        result = numer / total
+        span = n * rows // 4
+        done = []
+        for g in range(1):
+            piece = parts[g * (4 // 1):(g + 1) * (4 // 1)]
+            query = jnp.concatenate(piece, axis=0).astype(jnp.bfloat16)
+            scores = [
+                lax.dot_general(query, keys[c * span:(c + 1) * span], (((1,), (1,)), ((), ())),
+                                preferred_element_type=jnp.float32) + bias_row[0:1, c * span:(c + 1) * span]
+                for c in range(4)
+            ]
+            highest = functools.reduce(jnp.maximum, [jnp.max(x, axis=-1, keepdims=True) for x in scores])
+            total, numer = 0.0, 0.0
+            for c in range(4):
+                expo = jnp.exp(scores[c] - highest)
+                total = total + jnp.sum(expo, axis=-1, keepdims=True)
+                numer = numer + jnp.dot(expo.astype(jnp.bfloat16), keys[c * span:(c + 1) * span],
+                                        preferred_element_type=jnp.float32)
+            done.append(numer / total)
+        result = jnp.concatenate(done, axis=0)
         for i in range(2):
             top = result[i * rows:i * rows + half_rows]
             bottom = result[i * rows + half_rows:(i + 1) * rows]

time: 50.2 us -> 52.4 us (1.044)
  Pallas kernels: 45.3 us -> 47.6 us
    pallas_call x1, Pallas kernels: 45.3 us -> 47.6 us  [whole_kernel(): pl.pallas_call(functools.partial(fused, n), out_shape=jax.ShapeDtypeStruc...]
where the time goes in v2:
time: 52.4 us; the launch traced here: 52.2 us
  Pallas kernels  47.6 us (91%)
  local copies, waits for them, and re-layouts  2.02 us (4%)
  other arithmetic  1.32 us (3%)
  between operations  1.31 us (2%)
    pallas_call x1, Pallas kernels, whole_kernel(): pl.pallas_call(functools.partial(fused, n), out_shape=jax.ShapeDtypeStruc...  47.6 us
    pallas_call x1, local copies, waits for them, and re-layouts, whole_kernel(): pl.pallas_call(functools.partial(fused, n), out_shape=jax.ShapeDtypeStruc...  2.02 us
    broadcast_in_dim x1, other arithmetic, whole_kernel(): double = lambda gain: jnp.concatenate([gain, gain])[None, :]  1.32 us

profile of v2, /device:TPU:0, one launch (start us, length us, event | category | flops | bytes accessed | tf_op | source)
XLA Modules:
  0.0 52.2 jit_solution(544449717621286345)
XLA Ops:
  1.3 1.3 %maximum_bitcast_fusion = (f32[1,128]{1,0:T(1,128)}, f32[1,128]{1,0:T(1,128)}) fusion(f32[64]{0:T(128)} %param.11, f32[64]{0:T(128)} %param.12), kind=kLoop, calls=%fused_computation | loop fusion | flops 256 | bytes 1536 | tf_op jit(solution)/shard_map/broadcast_in_dim | solution.py:377
  2.6 47.6 %shard_map.82 = f32[128,960]{1,0:T(8,128)} custom-call(s32[1]{0:T(128)S(6)} %copy.10.count_ref, s32[1]{0:T(128)S(6)} %copy.11.block_ref, bf16[128,1920]{1,0:T(8,128)(2,1)} %bitcast.5, f32[6,1920]{1,0:T(8,128)} %mod_ref.1, bf16[3,1920,1024]{2,1,0:T(8,128)(2,1)} %w_ref.1, f32[1,128]{1,0:T(1,128)} %get-tuple-element.5.qg_ref, ...), custom_call_target="tpu_custom_call" | custom-call | tf_op jit(solution)/shard_map/pallas_call | solution.py:378
  50.2 2.0 %copy.9 = f32[128,960]{0,1:T(8,128)} copy(f32[128,960]{1,0:T(8,128)} %shard_map.82) | data formatting | bytes 983040 | tf_op jit(solution)/shard_map/pallas_call | solution.py:378
